TPU v7x, 8 devices: a whole 2x2x1 slice. The times are simulated.
8 devices in a mesh: dp: 1 (over z), tp: 2 (over y), cp: 4 (over x, core).
Axes of the slice: x: 2, y: 2, z: 1, core: 2. Of those that a mesh axis runs over, the one named last changes fastest.
Arguments:
- x: bfloat16 [4096, 2048], P(('dp', 'cp', 'tp'))
- w_q: bfloat16 [2048, 2048], P(None, 'tp')
- w_k: bfloat16 [2048, 256], P(None, 'tp')
- w_v: bfloat16 [2048, 256], P(None, 'tp')
- w_o: bfloat16 [2048, 2048], P('tp')
Outputs:
- output: bfloat16 [4096, 2048], P(('dp', 'cp', 'tp'))
All inputs are finite; a program needn't handle non-finite values.
Results may differ from a plain program's by a relative error of at most 0.00538824.
Values are sent between devices in bfloat16 or wider.
A program may use at most 1 GiB of HBM per device.

v0:
```python
import jax
import jax.numpy as jnp
from jax import lax
from jax.sharding import PartitionSpec as P

HEAD_DIM = 128


def block_scores(q_part, k_part):
    raw_scores = jnp.einsum("qhge,khe->hgqk", q_part, k_part, preferred_element_type=jnp.float32)
    return raw_scores * (HEAD_DIM ** -0.5)


def merge_block(soft_state, scores, v_part):
    run_max, run_sum, run_acc = soft_state
    new_max = jnp.maximum(run_max, scores.max(axis=-1))
    rescale = jnp.exp(run_max - new_max)
    p_block = jnp.exp(scores - new_max[..., None])
    new_sum = run_sum * rescale + p_block.sum(axis=-1)
    new_acc = run_acc * rescale[..., None] + jnp.einsum("hgqk,khe->hgqe", p_block.astype(jnp.bfloat16), v_part, preferred_element_type=jnp.float32)
    return new_max, new_sum, new_acc


def solution(mesh):
    cp_size = mesh.shape["cp"]
    row_spec = P(("dp", "cp", "tp"), None)

    def local_layer(x_loc, w_q, w_k, w_v, w_o):
        model_width = x_loc.shape[1]
        kv_local = w_k.shape[1] // HEAD_DIM
        group_size = w_q.shape[1] // w_k.shape[1]
        x_block = lax.all_gather(x_loc, "tp", axis=0, tiled=True)
        piece_len = x_block.shape[0] // 2
        q_all = jnp.dot(x_block, w_q, preferred_element_type=jnp.float32).astype(jnp.bfloat16).reshape(2, piece_len, kv_local, group_size, HEAD_DIM)
        k_all = jnp.dot(x_block, w_k, preferred_element_type=jnp.float32).astype(jnp.bfloat16).reshape(2, piece_len, kv_local, HEAD_DIM)
        v_all = jnp.dot(x_block, w_v, preferred_element_type=jnp.float32).astype(jnp.bfloat16).reshape(2, piece_len, kv_local, HEAD_DIM)
        q_low = q_all[0]
        q_high = q_all[1]
        cp_rank = lax.axis_index("cp")
        offsets = jnp.arange(piece_len)
        pos_low = cp_rank * piece_len + offsets
        pos_high = (2 * cp_size - 1 - cp_rank) * piece_len + offsets
        pos_both = jnp.concatenate([pos_low, pos_high])
        stat_shape = (kv_local, group_size, piece_len)
        empty_state = (jnp.full(stat_shape, -jnp.inf, jnp.float32), jnp.zeros(stat_shape, jnp.float32), jnp.zeros(stat_shape + (HEAD_DIM,), jnp.float32))
        k_flat = k_all.reshape(2 * piece_len, kv_local, HEAD_DIM)
        v_flat = v_all.reshape(2 * piece_len, kv_local, HEAD_DIM)
        low_scores = jnp.where(pos_low[:, None] >= pos_low[None, :], block_scores(q_low, k_all[0]), -jnp.inf)
        high_scores = jnp.where(pos_high[:, None] >= pos_both[None, :], block_scores(q_high, k_flat), -jnp.inf)
        own_states = (merge_block(empty_state, low_scores, v_all[0]), merge_block(empty_state, high_scores, v_flat))

        def earlier_source(states, kv_src):
            state_low, state_high = states
            k_src = kv_src[0, 0]
            v_src = kv_src[1, 0]
            return (merge_block(state_low, block_scores(q_low, k_src), v_src), merge_block(state_high, block_scores(q_high, k_src), v_src))

        def later_source(states, kv_src):
            state_low, state_high = states
            k_src = kv_src[0].reshape(2 * piece_len, kv_local, HEAD_DIM)
            v_src = kv_src[1].reshape(2 * piece_len, kv_local, HEAD_DIM)
            return (state_low, merge_block(state_high, block_scores(q_high, k_src), v_src))

        shift_pairs = [(dev_idx, (dev_idx + 1) % cp_size) for dev_idx in range(cp_size)]

        def kv_step(step_idx, loop_carry):
            states, kv_held = loop_carry
            kv_held = lax.ppermute(kv_held, "cp", shift_pairs)
            source = (cp_rank - step_idx) % cp_size
            states = lax.cond(source < cp_rank, earlier_source, later_source, states, kv_held)
            return states, kv_held

        kv_pair = jnp.stack([k_all, v_all])
        final_carry = lax.fori_loop(1, cp_size, kv_step, (own_states, kv_pair))
        state_low, state_high = final_carry[0]
        out_low = (state_low[2] / state_low[1][..., None]).astype(jnp.bfloat16)
        out_high = (state_high[2] / state_high[1][..., None]).astype(jnp.bfloat16)
        attn_out = jnp.stack([out_low, out_high], axis=2)
        w_o_heads = w_o.reshape(kv_local, group_size, HEAD_DIM, model_width)
        partial = jnp.einsum("hgsqe,hged->sqd", attn_out, w_o_heads, preferred_element_type=jnp.float32).reshape(2 * piece_len, model_width)
        y_loc = lax.psum_scatter(partial, "tp", scatter_dimension=0, tiled=True)
        return y_loc.astype(jnp.bfloat16)

    return jax.shard_map(local_layer, mesh=mesh, in_specs=(row_spec, P(None, "tp"), P(None, "tp"), P(None, "tp"), P("tp", None)), out_specs=row_spec, check_vma=False)
```

profile of v0, /device:TPU:0, one launch (start us, length us, event | category | flops | bytes accessed | tf_op | source)
XLA Modules:
  0.0 335.2 jit_solution(12977104952404836065)
XLA Ops:
  7.9 58.0 %all-gather.2.cloned.1.call-done = bf16[1024,2048]{1,0:T(8,128)(2,1)} async-done(((bf16[512,2048]{1,0:T(8,128)(2,1)}), bf16[1024,2048]{1,0:T(8,128)(2,1)}) %all-gather.2.cloned.1.call-update) | async-done | bytes 4194320 | tf_op jit(solution)/shard_map/all_gather | solution.py:32
  65.9 8.2 %convolution_convert_fusion = bf16[1024,1024]{0,1:T(8,128)(2,1)S(1)} fusion(bf16[1024,2048]{1,0:T(8,128)(2,1)} %all-gather.2.cloned.1.call-done, bf16[2048,1024]{1,0:T(8,128)(2,1)} %param.10), kind=kOutput, calls=%fused_computation.81 | convolution fusion | flops 4296015872 | bytes 10485760 | tf_op jit(solution)/shard_map/dot_general | solution.py:34
  75.5 7.4 %fusion.52 = (f32[8,512]{1,0:T(8,128)S(1)}, f32[1024,512,8]{1,0,2:T(8,128)}) fusion(pred[512,1024]{0,1:T(8,128)(4,1)S(1)} %broadcast_compare_fusion, bf16[512,8,128]{0,2,1:T(8,128)(2,1)S(1)} %bitcast.244, bf16[1024,128]{1,0:T(8,128)(2,1)S(1)} %convolution_convert_fusion.2), kind=kOutput, calls=%fused_computation.63 | convolution fusion | flops 1086320640 | bytes 18628608 | tf_op jit(solution)/shard_map/qhge,khe->hgqk/dot_general | solution.py:10
  82.9 9.2 %fusion.51 = f32[8,512]{1,0:T(8,128)S(1)} fusion(f32[1024,512,8]{1,0,2:T(8,128)} %get-tuple-element.426, f32[8,512]{1,0:T(8,128)S(1)} %get-tuple-element.425, pred[512,1024]{0,1:T(8,128)(4,1)S(1)} %broadcast_compare_fusion), kind=kLoop, calls=%fused_computation.62 | loop fusion | flops 16773120 | bytes 17334272 | tf_op jit(solution)/shard_map/reduce_sum | solution.py:19
  95.3 4.2 %convolution_convert_fusion.1 = bf16[1024,128]{1,0:T(8,128)(2,1)S(1)} fusion(bf16[1024,2048]{1,0:T(8,128)(2,1)} %all-gather.2.cloned.1.call-done, bf16[2048,128]{1,0:T(8,128)(2,1)S(1)} %copy-done.14), kind=kOutput, calls=%fused_computation.82 | convolution fusion | flops 537001984 | bytes 4980736 | tf_op jit(solution)/shard_map/dot_general | solution.py:36
  99.5 4.9 %add_bitcast_fusion = f32[1,8,512,128]{3,2,1,0:T(8,128)S(1)} fusion(f32[1024,512,8]{1,0,2:T(8,128)S(1)} %copy-done.3, f32[8,512]{1,0:T(8,128)S(1)} %get-tuple-element.425, pred[512,1024]{0,1:T(8,128)(4,1)S(1)} %broadcast_compare_fusion, f32[8,512]{1,0:T(8,128)S(1)} %exponential_multiply_fusion, bf16[1024,128]{1,0:T(8,128)(2,1)S(1)} %convolution_convert_fusion.1), kind=kOutput, calls=%fused_computation.79 | convolution fusion | flops 1091043328 | bytes 19693568 | tf_op jit(solution)/shard_map/hgqk,khe->hgqe/dot_general | solution.py:20
  113.4 105.2 %while.27 = (s32[]{:T(128)}, f32[1,8,512]{2,1,0:T(8,128)S(1)}, f32[1,8,512]{2,1,0:T(8,128)S(1)}, f32[1,8,512,128]{3,2,1,0:T(8,128)}, f32[1,8,512]{2,1,0:T(8,128)...) while((s32[]{:T(128)}, f32[1,8,512]{2,1,0:T(8,128)S(1)}, ...), condition=%wide.region_13.14_spmd, body=%wide.region_4.13_spmd.sunk | while | flops 2183159808 | bytes 86114952 | solution.py:74
  113.7 8.6 %collective-permute-done = bf16[2,2,512,1,128]{4,2,3,1,0:T(8,128)(2,1)S(1)} collective-permute-done((bf16[2,2,512,1,128]{4,2,3,1,0:T(8,128)(2,1)}, bf16[2,2,512,1,128]{4,2,3,1,0:T(8,128)(2,1)S(1)}, u32[]{:S(2)}, u32[]{:S(2)}) %collective-permute-start) | collective-permute-done | bytes 524320 | tf_op jit(solution)/shard_map/while/body/eval_jaxpr/ppermute | solution.py:68
  122.3 25.5 %conditional.2 = (f32[1,8,512]{2,1,0:T(8,128)S(1)}, f32[1,8,512]{2,1,0:T(8,128)S(1)}, f32[1,8,512,128]{3,2,1,0:T(8,128)}, f32[1,8,512]{2,1,0:T(8,128)S(1)}, f32[...) conditional(s32[]{:T(128)} %convert_element_type.91, (bf16[2,2,512,1,128]{4,2,3,1,0:T(8,128)(2,1)S(1)}, ...), branch_computations={%region_5.7_spmd, %region_8.12_spmd} | conditional | flops 2183159808 | bytes 82936008 | solution.py:70
  122.3 9.3 %bitcast_reduce_fusion = (f32[8,512]{1,0:T(8,128)S(1)}, f32[1024,512,8]{1,0,2:T(8,128)}) fusion(bf16[1024,128,1]{1,0,2:T(8,128)(2,1)S(1)} %bitcast.238, bf16[512,1,8,128]{3,0,2,1:T(8,128)(2,1)} %get-tuple-element.326), kind=kOutput, calls=%fused_computation.1 | convolution fusion | flops 1082126336 | bytes 18104320 | tf_op jit(solution)/shard_map/while/body/eval_jaxpr/cond/branch_0_fun/qhge,khe->hgqk/dot_general | solution.py:10
  131.6 8.5 %fusion.2 = f32[8,512]{1,0:T(8,128)S(1)} fusion(f32[1024,512,8]{1,0,2:T(8,128)} %get-tuple-element.414, f32[8,512]{1,0:T(8,128)S(1)} %bitcast.240), kind=kLoop, calls=%fused_computation.4 | loop fusion | flops 12578816 | bytes 16809984 | tf_op jit(solution)/shard_map/while/body/eval_jaxpr/cond/branch_0_fun/reduce_sum | solution.py:19
  140.1 7.6 %bitcast_add_fusion = f32[1,8,512,128]{3,2,1,0:T(8,128)S(1)} fusion(f32[1,8,512,128]{3,2,1,0:T(8,128)S(1)} %get-tuple-element.328, bf16[1024,128,1]{1,0,2:T(8,128)(2,1)S(1)} %bitcast.239, f32[1024,512,8]{1,0,2:T(8,128)} %get-tuple-element.414, f32[8,512]{1,0:T(8,128)S(1)} %bitcast.241, f32[8,512]{1,0:T(8,128)S(1)} %get-tuple-element.405), kind=kOutput, calls=%fused_computation.9 | convolution fusion | flops 1087373312 | bytes 21266432 | tf_op jit(solution)/shard_map/while/body/eval_jaxpr/cond/branch_0_fun/hgqk,khe->hgqe/dot_general | solution.py:20
  148.6 8.6 %collective-permute-done = bf16[2,2,512,1,128]{4,2,3,1,0:T(8,128)(2,1)S(1)} collective-permute-done((bf16[2,2,512,1,128]{4,2,3,1,0:T(8,128)(2,1)}, bf16[2,2,512,1,128]{4,2,3,1,0:T(8,128)(2,1)S(1)}, u32[]{:S(2)}, u32[]{:S(2)}) %collective-permute-start) | collective-permute-done | bytes 524320 | tf_op jit(solution)/shard_map/while/body/eval_jaxpr/ppermute | solution.py:68
  157.2 25.5 %conditional.2 = (f32[1,8,512]{2,1,0:T(8,128)S(1)}, f32[1,8,512]{2,1,0:T(8,128)S(1)}, f32[1,8,512,128]{3,2,1,0:T(8,128)}, f32[1,8,512]{2,1,0:T(8,128)S(1)}, f32[...) conditional(s32[]{:T(128)} %convert_element_type.91, (bf16[2,2,512,1,128]{4,2,3,1,0:T(8,128)(2,1)S(1)}, ...), branch_computations={%region_5.7_spmd, %region_8.12_spmd} | conditional | flops 2183159808 | bytes 82936008 | solution.py:70
  157.2 9.3 %bitcast_reduce_fusion = (f32[8,512]{1,0:T(8,128)S(1)}, f32[1024,512,8]{1,0,2:T(8,128)}) fusion(bf16[1024,128,1]{1,0,2:T(8,128)(2,1)S(1)} %bitcast.238, bf16[512,1,8,128]{3,0,2,1:T(8,128)(2,1)} %get-tuple-element.326), kind=kOutput, calls=%fused_computation.1 | convolution fusion | flops 1082126336 | bytes 18104320 | tf_op jit(solution)/shard_map/while/body/eval_jaxpr/cond/branch_0_fun/qhge,khe->hgqk/dot_general | solution.py:10
  166.5 8.5 %fusion.2 = f32[8,512]{1,0:T(8,128)S(1)} fusion(f32[1024,512,8]{1,0,2:T(8,128)} %get-tuple-element.414, f32[8,512]{1,0:T(8,128)S(1)} %bitcast.240), kind=kLoop, calls=%fused_computation.4 | loop fusion | flops 12578816 | bytes 16809984 | tf_op jit(solution)/shard_map/while/body/eval_jaxpr/cond/branch_0_fun/reduce_sum | solution.py:19
  175.0 7.6 %bitcast_add_fusion = f32[1,8,512,128]{3,2,1,0:T(8,128)S(1)} fusion(f32[1,8,512,128]{3,2,1,0:T(8,128)S(1)} %get-tuple-element.328, bf16[1024,128,1]{1,0,2:T(8,128)(2,1)S(1)} %bitcast.239, f32[1024,512,8]{1,0,2:T(8,128)} %get-tuple-element.414, f32[8,512]{1,0:T(8,128)S(1)} %bitcast.241, f32[8,512]{1,0:T(8,128)S(1)} %get-tuple-element.405), kind=kOutput, calls=%fused_computation.9 | convolution fusion | flops 1087373312 | bytes 21266432 | tf_op jit(solution)/shard_map/while/body/eval_jaxpr/cond/branch_0_fun/hgqk,khe->hgqe/dot_general | solution.py:20
  183.5 8.6 %collective-permute-done = bf16[2,2,512,1,128]{4,2,3,1,0:T(8,128)(2,1)S(1)} collective-permute-done((bf16[2,2,512,1,128]{4,2,3,1,0:T(8,128)(2,1)}, bf16[2,2,512,1,128]{4,2,3,1,0:T(8,128)(2,1)S(1)}, u32[]{:S(2)}, u32[]{:S(2)}) %collective-permute-start) | collective-permute-done | bytes 524320 | tf_op jit(solution)/shard_map/while/body/eval_jaxpr/ppermute | solution.py:68
  192.1 25.5 %conditional.2 = (f32[1,8,512]{2,1,0:T(8,128)S(1)}, f32[1,8,512]{2,1,0:T(8,128)S(1)}, f32[1,8,512,128]{3,2,1,0:T(8,128)}, f32[1,8,512]{2,1,0:T(8,128)S(1)}, f32[...) conditional(s32[]{:T(128)} %convert_element_type.91, (bf16[2,2,512,1,128]{4,2,3,1,0:T(8,128)(2,1)S(1)}, ...), branch_computations={%region_5.7_spmd, %region_8.12_spmd} | conditional | flops 2183159808 | bytes 82936008 | solution.py:70
  192.1 9.3 %bitcast_reduce_fusion = (f32[8,512]{1,0:T(8,128)S(1)}, f32[1024,512,8]{1,0,2:T(8,128)}) fusion(bf16[1024,128,1]{1,0,2:T(8,128)(2,1)S(1)} %bitcast.238, bf16[512,1,8,128]{3,0,2,1:T(8,128)(2,1)} %get-tuple-element.326), kind=kOutput, calls=%fused_computation.1 | convolution fusion | flops 1082126336 | bytes 18104320 | tf_op jit(solution)/shard_map/while/body/eval_jaxpr/cond/branch_0_fun/qhge,khe->hgqk/dot_general | solution.py:10
  201.4 8.5 %fusion.2 = f32[8,512]{1,0:T(8,128)S(1)} fusion(f32[1024,512,8]{1,0,2:T(8,128)} %get-tuple-element.414, f32[8,512]{1,0:T(8,128)S(1)} %bitcast.240), kind=kLoop, calls=%fused_computation.4 | loop fusion | flops 12578816 | bytes 16809984 | tf_op jit(solution)/shard_map/while/body/eval_jaxpr/cond/branch_0_fun/reduce_sum | solution.py:19
  210.0 7.6 %bitcast_add_fusion = f32[1,8,512,128]{3,2,1,0:T(8,128)S(1)} fusion(f32[1,8,512,128]{3,2,1,0:T(8,128)S(1)} %get-tuple-element.328, bf16[1024,128,1]{1,0,2:T(8,128)(2,1)S(1)} %bitcast.239, f32[1024,512,8]{1,0,2:T(8,128)} %get-tuple-element.414, f32[8,512]{1,0:T(8,128)S(1)} %bitcast.241, f32[8,512]{1,0:T(8,128)S(1)} %get-tuple-element.405), kind=kOutput, calls=%fused_computation.9 | convolution fusion | flops 1087373312 | bytes 21266432 | tf_op jit(solution)/shard_map/while/body/eval_jaxpr/cond/branch_0_fun/hgqk,khe->hgqe/dot_general | solution.py:20
  221.9 6.7 %convolution_bitcast_fusion = f32[1024,2048]{1,0:T(8,128)} fusion(bf16[1024,128,8]{1,0,2:T(8,128)(2,1)S(1)} %bitcast.253, bf16[8,128,2048]{2,1,0:T(8,128)(2,1)S(1)} %bitcast.257), kind=kOutput, calls=%fused_computation.72 | convolution fusion | flops 4294967296 | bytes 14680064 | tf_op jit(solution)/shard_map/hgsqe,hged->sqd/dot_general | solution.py:80
  228.6 95.5 %reduce-scatter.2.cloned.1.call-done = f32[512,2048]{1,0:T(8,128)} async-done(((f32[1024,2048]{1,0:T(8,128)}), f32[512,2048]{1,0:T(8,128)}) %reduce-scatter.2.cloned.1.call-update) | async-done | bytes 4194320 | tf_op jit(solution)/shard_map/reduce_scatter | solution.py:81
  (63 shorter events, 24.5 us)
Async XLA Ops:
  6.5 67.7 %copy-start = (bf16[2048,128]{1,0:T(8,128)(2,1)S(1)}, bf16[2048,128]{1,0:T(8,128)(2,1)}, u32[]{:S(2)}) copy-start(bf16[2048,128]{1,0:T(8,128)(2,1)} %param.11) | copy-start | bytes 1572868
  6.5 59.4 %all-gather.2.cloned.1.call-start = ((), (), s32[]{:S(2)}) async-start(), calls=%async_computation.1 | async-start | bytes 6291456 | tf_op jit(solution)/shard_map/all_gather | solution.py:32
  7.3 316.8 %reduce-scatter.2.cloned.1.call-start = ((), (), s32[]{:S(2)}) async-start(), calls=%async_computation.2 | async-start | bytes 12582912 | tf_op jit(solution)/shard_map/reduce_scatter | solution.py:81
  65.9 8.3 %copy-start.13 = (bf16[1024,2048]{1,0:T(8,128)(2,1)S(1)}, bf16[1024,2048]{1,0:T(8,128)(2,1)}, u32[]{:S(2)}) copy-start(bf16[1024,2048]{1,0:T(8,128)(2,1)} %all-gather.2.cloned.1.call-done) | copy-start | bytes 12582916
  74.2 8.7 %copy-start.8 = (bf16[512,1024]{0,1:T(8,128)(2,1)}, bf16[512,1024]{0,1:T(8,128)(2,1)S(1)}, u32[]{:S(2)}) copy-start(bf16[512,1024]{0,1:T(8,128)(2,1)S(1)} %get-tuple-element.421) | copy-start | bytes 3145732
  74.2 17.9 %copy-start.9 = (bf16[512,1024]{0,1:T(8,128)(2,1)}, bf16[512,1024]{0,1:T(8,128)(2,1)S(1)}, u32[]{:S(2)}) copy-start(bf16[512,1024]{0,1:T(8,128)(2,1)S(1)} %get-tuple-element.422) | copy-start | bytes 3145732
  75.5 16.6 %copy-start.10 = (bf16[1024,128]{1,0:T(8,128)(2,1)}, bf16[1024,128]{1,0:T(8,128)(2,1)S(1)}, u32[]{:S(2)}) copy-start(bf16[1024,128]{1,0:T(8,128)(2,1)S(1)} %convolution_convert_fusion.2) | copy-start | bytes 786436
  92.2 3.2 copy-start.14
  92.2 7.4 %copy-start.3 = (f32[1024,512,8]{1,0,2:T(8,128)S(1)}, f32[1024,512,8]{1,0,2:T(8,128)}, u32[]{:S(2)}) copy-start(f32[1024,512,8]{1,0,2:T(8,128)} %get-tuple-element.426) | copy-start | bytes 50331652
  104.4 8.2 %copy-start.11 = (bf16[1024,128]{1,0:T(8,128)(2,1)S(1)}, bf16[1024,128]{1,0:T(8,128)(2,1)}, u32[]{:S(2)}) copy-start(bf16[1024,128]{1,0:T(8,128)(2,1)} %copy-done.10) | copy-start | bytes 786436
  113.6 8.6 %collective-permute-start = (bf16[2,2,512,1,128]{4,2,3,1,0:T(8,128)(2,1)}, bf16[2,2,512,1,128]{4,2,3,1,0:T(8,128)(2,1)S(1)}, u32[]{:S(2)}, u32[]{:S(2)}) collective-permute-start(bf16[2,2,512,1,128]{4,2,3,1,0:T(8,128)(2,1)} %get-tuple-element.542), channel_id=1, source_target_pairs={{0,1},{1,2},{2,3},{3,0},{4,5},{5,6},{6,7},{7,4}} | collective-permute-start | bytes 1572872 | tf_op jit(solution)/shard_map/while/body/eval_jaxpr/ppermute | solution.py:68
  148.6 8.6 %collective-permute-start = (bf16[2,2,512,1,128]{4,2,3,1,0:T(8,128)(2,1)}, bf16[2,2,512,1,128]{4,2,3,1,0:T(8,128)(2,1)S(1)}, u32[]{:S(2)}, u32[]{:S(2)}) collective-permute-start(bf16[2,2,512,1,128]{4,2,3,1,0:T(8,128)(2,1)} %get-tuple-element.542), channel_id=1, source_target_pairs={{0,1},{1,2},{2,3},{3,0},{4,5},{5,6},{6,7},{7,4}} | collective-permute-start | bytes 1572872 | tf_op jit(solution)/shard_map/while/body/eval_jaxpr/ppermute | solution.py:68
  183.5 8.6 %collective-permute-start = (bf16[2,2,512,1,128]{4,2,3,1,0:T(8,128)(2,1)}, bf16[2,2,512,1,128]{4,2,3,1,0:T(8,128)(2,1)S(1)}, u32[]{:S(2)}, u32[]{:S(2)}) collective-permute-start(bf16[2,2,512,1,128]{4,2,3,1,0:T(8,128)(2,1)} %get-tuple-element.542), channel_id=1, source_target_pairs={{0,1},{1,2},{2,3},{3,0},{4,5},{5,6},{6,7},{7,4}} | collective-permute-start | bytes 1572872 | tf_op jit(solution)/shard_map/while/body/eval_jaxpr/ppermute | solution.py:68
  218.6 3.2 copy-start.12
  221.9 106.0 %copy-start.1 = (bf16[2048,128]{1,0:T(8,128)(2,1)S(1)}, bf16[2048,128]{1,0:T(8,128)(2,1)}, u32[]{:S(2)}) copy-start(bf16[2048,128]{1,0:T(8,128)(2,1)} %param.11) | copy-start | bytes 1572868
Sparse Core Ops, SparseCore 0:
  8.8 57.0 all-gather.1
  228.7 95.3 reduce-scatter.1
where the time goes:
time: 341 us; the launch traced here: 335 us
  waiting for transfers between devices  180 us (53%)
  matrix products  88.3 us (26%)
  other arithmetic  44.8 us (13%)
  between operations  14.1 us (4%)
  local copies, waits for them, and re-layouts  7.35 us (2%)
    reduce_scatter x1, waiting for transfers between devices, local_layer(): y_loc = lax.psum_scatter(partial, 'tp', scatter_dimension=0, tiled=True)  95.5 us
    all_gather x1, waiting for transfers between devices, local_layer(): x_block = lax.all_gather(x_loc, 'tp', axis=0, tiled=True)  58 us
    dot_general x5, matrix products, block_scores(): jnp.einsum('qhge,khe->hgqk', q_part, k_part, preferred_element_type=jnp.f...  36.7 us
    reduce_sum x5, other arithmetic, merge_block(): new_sum = run_sum * rescale + p_block.sum(axis=-1)  36.4 us
    dot_general x5, matrix products, merge_block(): jnp.einsum('hgqk,khe->hgqe', p_block.astype(jnp.bfloat16), v_part, prefer...  31.3 us
    ppermute x3, waiting for transfers between devices, kv_step(): kv_held = lax.ppermute(kv_held, 'cp', shift_pairs)  25.8 us
    dot_general x1, matrix products, local_layer(): jnp.dot(x_block, w_q, preferred_element_type=jnp.float32)  8.17 us
  transfers between devices with their start and end apart: 5, of which 5 were waited for; matrix products, arithmetic and copies ran while one was open for 0% of the time, Pallas kernels for 0%

commit v1 on v0

v1 whole, which is shorter than its diff:
```python
import functools

import jax
import jax.numpy as jnp
from jax import lax
from jax.experimental import pallas as pl
from jax.experimental.pallas import tpu as pltpu
from jax.sharding import PartitionSpec as P

HD = 128
R = 512
MESH = pl.DeviceIdType.MESH
F32 = jnp.float32
BF16 = jnp.bfloat16
EXP2_SCALE = (HD ** -0.5) * 1.4426950408889634
N_ITEMS = 13


def dot_nt(a, b):
    return lax.dot_general(a, b, (((1,), (1,)), ((), ())), preferred_element_type=F32)


def dot_nn(a, b):
    return jnp.dot(a, b, preferred_element_type=F32)


def kernel(x_hbm, wq_hbm, wk_hbm, wv_hbm, wo_hbm, out_ref,
           xs, wkv_n, wq_n, wo_n, a_f, wo_f, kvb, qb, ob, m_st, l_st, acc_st, yacc,
           lsem, ys, yr, xsnd, xr, d1s, d1r, d2s, d2r, kvr, kvs):
    dp = lax.axis_index("dp")
    tp = lax.axis_index("tp")
    cp = lax.axis_index("cp")
    xc = cp // 2
    core = cp % 2
    cp_sib = cp + 1 - 2 * core
    cp_x = (cp + 2) % 4
    cp_xs = (cp_sib + 2) % 4
    sib = (dp, tp, cp_sib)
    xn = (dp, tp, cp_x)
    yn = (dp, 1 - tp, cp)
    dg = (dp, 1 - tp, cp_x)
    far = 1 - tp

    def piece_of(c):
        return c + tp * (7 - 2 * c)

    p = piece_of(cp)
    p_sib = piece_of(cp_sib)
    p_x = piece_of(cp_x)
    p_xs = piece_of(cp_xs)
    is_h = tp == 1
    is_l = tp == 0
    x_sends = xc == tp
    x_gets = xc != tp

    def load(i, src, dst):
        return pltpu.make_async_copy(src, dst, lsem.at[i])

    loads = [load(0, x_hbm, xs),
             load(1, wk_hbm, wkv_n.at[:, pl.ds(0, HD)]),
             load(2, wv_hbm, wkv_n.at[:, pl.ds(HD, HD)])]
    loads += [load(3 + j, wq_hbm.at[:, pl.ds(256 * j, 256)], wq_n.at[j]) for j in range(4)]
    loads += [load(7, wo_hbm, wo_n)]
    for cpy in loads:
        cpy.start()

    bar = pltpu.get_barrier_semaphore()
    for dev in (sib, xn, yn, dg):
        pl.semaphore_signal(bar, 1, device_id=dev, device_id_type=MESH)
    pl.semaphore_wait(bar, 4)

    def remote(src, dst, ss, rs, dev):
        return pltpu.make_async_remote_copy(src, dst, ss, rs, device_id=dev, device_id_type=MESH)

    def quarter(k, q):
        if isinstance(k, int) and k == 0:
            return [a_f.at[0, pl.ds(q * 512, 512), :]]
        if isinstance(k, int) and k < 5:
            return [a_f.at[k, pl.ds(q * 512, 512), :]]
        return [wo_f.at[k - 5, pl.ds(q * 32, 32), :]]

    def y_send(k):
        q = cp
        if isinstance(k, int) and k == 0:
            rows = pl.ds(q * 512, 512)
            return [remote(wk_hbm.at[rows, :], a_f.at[0, rows, pl.ds(0, HD)], ys.at[0], yr.at[0], yn),
                    remote(wv_hbm.at[rows, :], a_f.at[0, rows, pl.ds(HD, HD)], ys.at[13], yr.at[13], yn)]
        if isinstance(k, int) and k < 5:
            rows = pl.ds(q * 512, 512)
            return [remote(wq_hbm.at[rows, pl.ds(256 * (k - 1), 256)], a_f.at[k, rows, :], ys.at[k], yr.at[k], yn)]
        return [remote(wo_hbm.at[pl.ds((k - 5) * HD + q * 32, 32), :], wo_f.at[k - 5, pl.ds(q * 32, 32), :],
                       ys.at[k], yr.at[k], yn)]

    def x_fwd(k):
        r = quarter(k, cp)[0]
        return remote(r, r, xsnd.at[k], xr.at[k], xn)

    def x_in(k):
        r = quarter(k, cp_x)[0]
        return remote(r, r, xsnd.at[k], xr.at[k], xn)

    def d1_fwd(k):
        r = quarter(k, cp)[0]
        return remote(r, r, d1s.at[k], d1r.at[k], sib)

    def d1_in(k):
        r = quarter(k, cp_sib)[0]
        return remote(r, r, d1s.at[k], d1r.at[k], sib)

    def d2_fwd(k):
        r = quarter(k, cp_x)[0]
        return remote(r, r, d2s.at[k], d2r.at[k], sib)

    def d2_in(k):
        r = quarter(k, cp_xs)[0]
        return remote(r, r, d2s.at[k], d2r.at[k], sib)

    def start_y(k):
        for c in y_send(k):
            c.start()

    def relay_y(k):
        for c in y_send(k):
            c.wait_recv()
        x_fwd(k).start()
        d1_fwd(k).start()

    def relay_x(k):
        x_in(k).wait_recv()
        d2_fwd(k).start()

    def ready(k):
        d1_in(k).wait_recv()
        d2_in(k).wait_recv()

    def kv_ref(piece, e):
        return kvb.at[e, pl.ds(piece * R, R), :]

    def kv_copy(piece, e, ssem, dev):
        r = kv_ref(piece, e)
        return remote(r, r, ssem, kvr.at[piece, e], dev)

    def kv_wait(piece, e):
        kv_copy(piece, e, kvs.at[0], sib).wait_recv()

    def own_kv_sends(e, slot, diag):
        kv_copy(p, e, kvs.at[slot], sib).start()

        @pl.when(x_sends)
        def _():
            kv_copy(p, e, kvs.at[2 + slot], xn).start()

        @pl.when(is_l)
        def _():
            kv_copy(p, e, kvs.at[4 + slot], yn).start()
            if diag:
                kv_copy(p, e, kvs.at[6], dg).start()

    def project(w):
        return dot_nn(xs[...], w).astype(BF16)

    def kv_project(w, e):
        kvb[e, pl.ds(pl.multiple_of(p * R, R), R), :] = project(w)

    def soft_new(h, rows, s, v):
        m = jnp.max(s, axis=-1, keepdims=True)
        pr = jnp.exp2((s - m) * EXP2_SCALE)
        n = s.shape[1]
        l = pr[:, 0:128]
        for t in range(1, n // 128):
            l = l + pr[:, t * 128:(t + 1) * 128]
        m_st[h, rows, :] = jnp.broadcast_to(m, (m.shape[0], 128))
        l_st[h, rows, :] = l
        acc_st[h, rows, :] = dot_nn(pr.astype(BF16), v)

    def soft_add(h, rows, s, v):
        m_old = m_st[h, rows, :]
        m_new = jnp.maximum(m_old, jnp.max(s, axis=-1, keepdims=True))
        alpha = jnp.exp2((m_old - m_new) * EXP2_SCALE)
        n = s.shape[1]
        parts = [jnp.exp2((s[:, t * 128:(t + 1) * 128] - m_new) * EXP2_SCALE) for t in range(n // 128)]
        l = parts[0]
        for t in range(1, n // 128):
            l = l + parts[t]
        pr = jnp.concatenate(parts, axis=1)
        m_st[h, rows, :] = m_new
        l_st[h, rows, :] = l_st[h, rows, :] * alpha + l
        acc_st[h, rows, :] = acc_st[h, rows, :] * alpha + dot_nn(pr.astype(BF16), v)

    def att_self(h, qi, e):
        base = pl.multiple_of(p * R, R)
        k_lo = kvb[e, pl.ds(base, 256), 0:HD]
        v_lo = kvb[e, pl.ds(base, 256), HD:2 * HD]
        k_all = kvb[e, pl.ds(base, R), 0:HD]
        v_all = kvb[e, pl.ds(base, R), HD:2 * HD]
        row = lax.broadcasted_iota(jnp.int32, (256, 256), 0)
        col = lax.broadcasted_iota(jnp.int32, (256, 256), 1)
        s = dot_nt(qb[qi, 0:256, :], k_lo)
        soft_new(h, slice(0, 256), jnp.where(row >= col, s, -jnp.inf), v_lo)
        row2 = lax.broadcasted_iota(jnp.int32, (256, 512), 0) + 256
        col2 = lax.broadcasted_iota(jnp.int32, (256, 512), 1)
        s = dot_nt(qb[qi, 256:512, :], k_all)
        soft_new(h, slice(256, 512), jnp.where(row2 >= col2, s, -jnp.inf), v_all)

    def att_piece(h, qi, e, piece):
        base = pl.multiple_of(piece * R, R)
        k = kvb[e, pl.ds(base, R), 0:HD]
        v = kvb[e, pl.ds(base, R), HD:2 * HD]
        for c in range(2):
            rows = slice(256 * c, 256 * c + 256)
            soft_add(h, rows, dot_nt(qb[qi, rows, :], k), v)

    def finish_head(h, oi):
        l = jnp.sum(l_st[h], axis=-1, keepdims=True)
        ob[oi] = (acc_st[h] / l).astype(BF16)

    start_y(0)
    start_y(1)
    loads[0].wait()
    loads[1].wait()
    loads[2].wait()
    kv_project(wkv_n[...], tp)
    own_kv_sends(tp, 0, False)

    for j in range(4):
        loads[3 + j].wait()

    def q_near(j, carry):
        r = project(wq_n[j])
        qb[2 * j] = r[:, 0:HD]
        qb[2 * j + 1] = r[:, HD:2 * HD]
        return carry

    lax.fori_loop(0, 4, q_near, 0)

    def near_self(h, carry):
        att_self(h, h, tp)
        return carry

    lax.fori_loop(0, 8, near_self, 0)

    relay_y(0)
    start_y(2)

    kv_wait(p_sib, tp)

    def near_range(lo, hi):
        n = hi - lo

        def body(i, carry):
            att_piece(i // n, i // n, tp, lo + i % n)
            return carry

        lax.fori_loop(0, 8 * n, body, 0)

    @pl.when(p_sib < p)
    def _():
        def body(h, carry):
            att_piece(h, h, tp, p_sib)
            return carry

        lax.fori_loop(0, 8, body, 0)

    relay_y(1)
    start_y(3)
    relay_x(0)

    @pl.when(x_gets)
    def _():
        kv_wait(p_x, tp)
        kv_copy(p_x, tp, kvs.at[7], sib).start()
        kv_wait(p_xs, tp)

        def body(i, carry):
            att_piece(i // 2, i // 2, tp, lax.min(p_x, p_xs) + i % 2)
            return carry

        lax.fori_loop(0, 16, body, 0)

    ready(0)
    kv_project(a_f[0], far)
    own_kv_sends(far, 1, True)

    relay_y(2)
    start_y(4)
    relay_x(1)

    @pl.when(is_h)
    def _():
        kv_wait(cp, 0)
        kv_copy(cp, 0, kvs.at[11], xn).start()
        kv_copy(cp, 0, kvs.at[9], sib).start()
        kv_wait(cp_x, 0)
        kv_copy(cp_x, 0, kvs.at[12], sib).start()

    @pl.when(x_gets)
    def _():
        kv_wait(p_x, far)
        kv_copy(p_x, far, kvs.at[8], sib).start()

    kv_wait(p_sib, far)

    @pl.when(x_gets)
    def _():
        kv_wait(p_xs, far)

    @pl.when(is_h)
    def _():
        kv_wait(cp_sib, 0)
        kv_wait(cp_xs, 0)

    def far_q(j):
        r = project(a_f[1 + j])
        qb[8 + 2 * j] = r[:, 0:HD]
        qb[9 + 2 * j] = r[:, HD:2 * HD]

    def far_head(hf):
        att_self(hf, 8 + hf, far)

        def body(i, carry):
            att_piece(hf, 8 + hf, far, i)
            return carry

        lax.fori_loop(0, p, body, 0)
        finish_head(hf, 8 + hf)

    def far_head_slot(hf, slot):
        att_self(slot, 8 + hf, far)

        def body(i, carry):
            att_piece(slot, 8 + hf, far, i)
            return carry

        lax.fori_loop(0, p, body, 0)
        finish_head(slot, 8 + hf)

    ready(1)
    far_q(0)

    def far0(i, carry):
        far_head_slot(i, 8 + i % 2)
        return carry

    lax.fori_loop(0, 2, far0, 0)

    relay_y(3)
    start_y(5)
    start_y(6)
    relay_x(2)

    @pl.when(is_h)
    def _():
        kv_wait(cp, 1)
        kv_copy(cp, 1, kvs.at[10], sib).start()
        kv_wait(cp_x, 1)
        kv_copy(cp_x, 1, kvs.at[13], sib).start()
        kv_wait(cp_sib, 1)
        kv_wait(cp_xs, 1)

        def body(i, carry):
            att_piece(i // 4, i // 4, 1, i % 4)
            return carry

        lax.fori_loop(0, 16, body, 0)

    relay_y(4)
    start_y(7)
    start_y(8)
    relay_x(3)

    @pl.when(is_h)
    def _():
        def body(i, carry):
            att_piece(i // 4, i // 4, 1, i % 4)
            return carry

        lax.fori_loop(16, 32, body, 0)

    def near_finish(h, carry):
        finish_head(h, h)
        return carry

    lax.fori_loop(0, 8, near_finish, 0)

    loads[7].wait()

    def near_out(t, carry):
        cols = pl.ds(pl.multiple_of(t * 512, 512), 512)
        o_all = jnp.concatenate([ob[i] for i in range(8)], axis=1)
        yacc[:, cols] = dot_nn(o_all, wo_n[:, cols])
        return carry

    lax.fori_loop(0, 4, near_out, 0)

    def far_rest(i, carry):
        hf = i + 2

        @pl.when(i == 0)
        def _():
            relay_x(4)

        @pl.when(i > 0)
        def _():
            relay_x(4 + i)

        relay_y(5 + i)

        @pl.when(i < 4)
        def _():
            start_y(9 + i)

        @pl.when(i % 2 == 0)
        def _():
            j = hf // 2
            rd = a_f.at[1 + j, pl.ds(cp_sib * 512, 512), :]
            remote(rd, rd, d1s.at[1 + j], d1r.at[1 + j], sib).wait_recv()
            rd2 = a_f.at[1 + j, pl.ds(cp_xs * 512, 512), :]
            remote(rd2, rd2, d2s.at[1 + j], d2r.at[1 + j], sib).wait_recv()
            far_q(j)

        far_head_slot(hf, 8 + i % 2)
        return carry

    lax.fori_loop(0, 6, far_rest, 0)

    def far_out(j, last):
        ready(5 + 2 * j)
        ready(6 + 2 * j)

        def body(t, carry):
            cols = pl.ds(pl.multiple_of(t * 512, 512), 512)
            o_pair = jnp.concatenate([ob[8 + 2 * j], ob[9 + 2 * j]], axis=1)
            w = jnp.concatenate([wo_f[2 * j, :, cols], wo_f[2 * j + 1, :, cols]], axis=0)
            r = yacc[:, cols] + dot_nn(o_pair, w)
            if last:
                out_ref[:, cols] = r.astype(BF16)
            else:
                yacc[:, cols] = r
            return carry

        lax.fori_loop(0, 4, body, 0)

    relay_y(11)
    relay_x(10)
    far_out(0, False)
    relay_y(12)
    relay_x(11)
    far_out(1, False)
    relay_x(12)
    far_out(2, False)
    far_out(3, True)

    for k in range(5):
        for c in y_send(k):
            c.wait_send()
        x_fwd(k).wait_send()
        d1_fwd(k).wait_send()
        d2_fwd(k).wait_send()

    def drain(k, carry):
        for c in y_send(k):
            c.wait_send()
        x_fwd(k).wait_send()
        d1_fwd(k).wait_send()
        d2_fwd(k).wait_send()
        return carry

    lax.fori_loop(5, N_ITEMS, drain, 0)

    def sent(piece, e, slot, dev):
        kv_copy(piece, e, kvs.at[slot], dev).wait_send()

    sent(p, tp, 0, sib)
    sent(p, far, 1, sib)

    @pl.when(x_sends)
    def _():
        sent(p, tp, 2, xn)
        sent(p, far, 3, xn)

    @pl.when(x_gets)
    def _():
        sent(p_x, tp, 7, sib)
        sent(p_x, far, 8, sib)

    @pl.when(is_l)
    def _():
        sent(p, tp, 4, yn)
        sent(p, far, 5, yn)
        sent(p, far, 6, dg)

    @pl.when(is_h)
    def _():
        sent(cp, 0, 9, sib)
        sent(cp, 1, 10, sib)
        sent(cp, 0, 11, xn)
        sent(cp_x, 0, 12, sib)
        sent(cp_x, 1, 13, sib)


def solution(mesh):
    row_spec = P(("dp", "cp", "tp"), None)

    def local_layer(x_loc, w_q, w_k, w_v, w_o):
        anyspec = pl.BlockSpec(memory_space=pl.ANY)
        dma = pltpu.SemaphoreType.DMA
        return pl.pallas_call(
            kernel,
            out_shape=jax.ShapeDtypeStruct((R, 2048), BF16),
            in_specs=[anyspec] * 5,
            out_specs=pl.BlockSpec(memory_space=pltpu.VMEM),
            scratch_shapes=[
                pltpu.VMEM((R, 2048), BF16),
                pltpu.VMEM((2048, 256), BF16),
                pltpu.VMEM((4, 2048, 256), BF16),
                pltpu.VMEM((1024, 2048), BF16),
                pltpu.VMEM((5, 2048, 256), BF16),
                pltpu.VMEM((8, 128, 2048), BF16),
                pltpu.VMEM((2, 4096, 256), BF16),
                pltpu.VMEM((16, R, HD), BF16),
                pltpu.VMEM((16, R, HD), BF16),
                pltpu.VMEM((10, R, 128), F32),
                pltpu.VMEM((10, R, 128), F32),
                pltpu.VMEM((10, R, 128), F32),
                pltpu.VMEM((R, 2048), F32),
                dma((8,)),
                dma((14,)), dma((14,)),
                dma((13,)), dma((13,)),
                dma((13,)), dma((13,)),
                dma((13,)), dma((13,)),
                dma((8, 2)), dma((14,)),
            ],
            compiler_params=pltpu.CompilerParams(
                collective_id=0, has_side_effects=True, vmem_limit_bytes=62 * 1024 * 1024),
            name="attn_all",
        )(x_loc, w_q, w_k, w_v, w_o)

    return jax.shard_map(local_layer, mesh=mesh,
                         in_specs=(row_spec, P(None, "tp"), P(None, "tp"), P(None, "tp"), P("tp", None)),
                         out_specs=row_spec, check_vma=False)
```

time: 341 us -> 143 us (0.42)
  the two profiles are of different devices: /device:TPU:0 before, /device:TPU:5 now
where the time goes in v1:
time: 143 us; the launch traced here: 140 us
  Pallas kernels  137 us (96%)
  local copies, waits for them, and re-layouts  3.16 us (2%)
    pallas_call x1, Pallas kernels, local_layer(): pl.pallas_call(kernel, out_shape=jax.ShapeDtypeStruct((R, 2048), BF16), i...  137 us
    unnamed x1, local copies, waits for them, and re-layouts  3.16 us

profile of v1, /device:TPU:5, one launch (start us, length us, event | category | flops | bytes accessed | tf_op | source)
XLA Modules:
  0.0 140.5 jit_solution(1333444420023568053)
XLA Ops:
  0.0 137.3 %attn_all.1 = bf16[512,2048]{1,0:T(8,128)(2,1)} custom-call(bf16[512,2048]{1,0:T(8,128)(2,1)} %x_hbm.1, bf16[2048,1024]{1,0:T(8,128)(2,1)} %wq_hbm.1, bf16[2048,128]{1,0:T(8,128)(2,1)} %wk_hbm.1, bf16[2048,128]{1,0:T(8,128)(2,1)} %wv_hbm.1, bf16[1024,2048]{1,0:T(8,128)(2,1)} %wo_hbm.1), custom_call_target="tpu_custom_call" | custom-call | tf_op jit(solution)/shard_map/attn_all/pallas_call | solution.py:507
  137.3 3.2 %copy.7 = bf16[512,2048]{1,0:T(8,128)(2,1)} copy(bf16[512,2048]{1,0:T(8,128)(2,1)} %attn_all.1) | data formatting | bytes 4194304

commit v2 on v1

--- a/solution.py
+++ b/solution.py
@@ -162,65 +162,82 @@
     def kv_project(w, e):
         kvb[e, pl.ds(pl.multiple_of(p * R, R), R), :] = project(w)
 
-    def soft_new(h, rows, s, v):
+    def exp_scaled(d):
+        return jnp.exp2(d * EXP2_SCALE)
+
+    def soft_new(slot, rows, s, v):
         m = jnp.max(s, axis=-1, keepdims=True)
-        pr = jnp.exp2((s - m) * EXP2_SCALE)
-        n = s.shape[1]
-        l = pr[:, 0:128]
-        for t in range(1, n // 128):
-            l = l + pr[:, t * 128:(t + 1) * 128]
-        m_st[h, rows, :] = jnp.broadcast_to(m, (m.shape[0], 128))
-        l_st[h, rows, :] = l
-        acc_st[h, rows, :] = dot_nn(pr.astype(BF16), v)
-
-    def soft_add(h, rows, s, v):
-        m_old = m_st[h, rows, :]
+        parts = [exp_scaled(s[:, t:t + 128] - m) for t in range(0, s.shape[1], 128)]
+        m_st[slot, rows, :] = jnp.broadcast_to(m, (m.shape[0], 128))
+        l_st[slot, rows, :] = functools.reduce(jnp.add, parts)
+        acc_st[slot, rows, :] = dot_nn(jnp.concatenate([t.astype(BF16) for t in parts], axis=1), v)
+
+    def soft_add(slot, s, v):
+        m_old = m_st[slot]
         m_new = jnp.maximum(m_old, jnp.max(s, axis=-1, keepdims=True))
-        alpha = jnp.exp2((m_old - m_new) * EXP2_SCALE)
-        n = s.shape[1]
-        parts = [jnp.exp2((s[:, t * 128:(t + 1) * 128] - m_new) * EXP2_SCALE) for t in range(n // 128)]
-        l = parts[0]
-        for t in range(1, n // 128):
-            l = l + parts[t]
-        pr = jnp.concatenate(parts, axis=1)
-        m_st[h, rows, :] = m_new
-        l_st[h, rows, :] = l_st[h, rows, :] * alpha + l
-        acc_st[h, rows, :] = acc_st[h, rows, :] * alpha + dot_nn(pr.astype(BF16), v)
-
-    def att_self(h, qi, e):
+        alpha = exp_scaled(m_old - m_new)
+        parts = [exp_scaled(s[:, t:t + 128] - m_new) for t in range(0, s.shape[1], 128)]
+        m_st[slot] = m_new
+        l_st[slot] = l_st[slot] * alpha + functools.reduce(jnp.add, parts)
+        pr = jnp.concatenate([t.astype(BF16) for t in parts], axis=1)
+        acc_st[slot] = acc_st[slot] * alpha + dot_nn(pr, v)
+
+    def att_self(slot, qi, e):
         base = pl.multiple_of(p * R, R)
-        k_lo = kvb[e, pl.ds(base, 256), 0:HD]
-        v_lo = kvb[e, pl.ds(base, 256), HD:2 * HD]
-        k_all = kvb[e, pl.ds(base, R), 0:HD]
-        v_all = kvb[e, pl.ds(base, R), HD:2 * HD]
+        k = kvb[e, pl.ds(base, R), 0:HD]
+        v = kvb[e, pl.ds(base, R), HD:2 * HD]
         row = lax.broadcasted_iota(jnp.int32, (256, 256), 0)
         col = lax.broadcasted_iota(jnp.int32, (256, 256), 1)
-        s = dot_nt(qb[qi, 0:256, :], k_lo)
-        soft_new(h, slice(0, 256), jnp.where(row >= col, s, -jnp.inf), v_lo)
+        s = dot_nt(qb[qi, 0:256, :], k[0:256])
+        soft_new(slot, slice(0, 256), jnp.where(row >= col, s, -jnp.inf), v[0:256])
         row2 = lax.broadcasted_iota(jnp.int32, (256, 512), 0) + 256
         col2 = lax.broadcasted_iota(jnp.int32, (256, 512), 1)
-        s = dot_nt(qb[qi, 256:512, :], k_all)
-        soft_new(h, slice(256, 512), jnp.where(row2 >= col2, s, -jnp.inf), v_all)
-
-    def att_piece(h, qi, e, piece):
+        s = dot_nt(qb[qi, 256:512, :], k)
+        soft_new(slot, slice(256, 512), jnp.where(row2 >= col2, s, -jnp.inf), v)
+
+    def att_tile(slot, qi, e, piece, n_pieces):
         base = pl.multiple_of(piece * R, R)
-        k = kvb[e, pl.ds(base, R), 0:HD]
-        v = kvb[e, pl.ds(base, R), HD:2 * HD]
-        for c in range(2):
-            rows = slice(256 * c, 256 * c + 256)
-            soft_add(h, rows, dot_nt(qb[qi, rows, :], k), v)
-
-    def finish_head(h, oi):
-        l = jnp.sum(l_st[h], axis=-1, keepdims=True)
-        ob[oi] = (acc_st[h] / l).astype(BF16)
+        k = kvb[e, pl.ds(base, n_pieces * R), 0:HD]
+        v = kvb[e, pl.ds(base, n_pieces * R), HD:2 * HD]
+        for u in range(2):
+            soft_add(slot + u, dot_nt(qb[qi + u], k), v)
+
+    def finish_head(slot, oi):
+        l = jnp.sum(l_st[slot], axis=-1, keepdims=True)
+        ob[oi] = (acc_st[slot] / l).astype(BF16)
+
+    def dyn(k, fn):
+        @pl.when(k < 5)
+        def _():
+            fn(k, lambda q: a_f.at[k, pl.ds(q * 512, 512), :])
+
+        @pl.when(k >= 5)
+        def _():
+            fn(k, lambda q: wo_f.at[k - 5, pl.ds(q * 32, 32), :])
+
+    def ry(k):
+        def fn(k, at):
+            r = at(cp)
+            remote(r, r, ys.at[k], yr.at[k], yn).wait_recv()
+            remote(r, r, xsnd.at[k], xr.at[k], xn).start()
+            remote(r, r, d1s.at[k], d1r.at[k], sib).start()
+        dyn(k, fn)
+
+    def rx(k):
+        def fn(k, at):
+            r = at(cp_x)
+            remote(r, r, xsnd.at[k], xr.at[k], xn).wait_recv()
+            remote(r, r, d2s.at[k], d2r.at[k], sib).start()
+        dyn(k, fn)
 
     start_y(0)
-    start_y(1)
     loads[0].wait()
     loads[1].wait()
     loads[2].wait()
     kv_project(wkv_n[...], tp)
     own_kv_sends(tp, 0, False)
+    start_y(1)
+    start_y(2)
 
     for j in range(4):
         loads[3 + j].wait()
@@ -233,36 +250,30 @@
 
     lax.fori_loop(0, 4, q_near, 0)
 
-    def near_self(h, carry):
-        att_self(h, h, tp)
-        return carry
-
-    lax.fori_loop(0, 8, near_self, 0)
+    def near_self(i, carry):
+        att_self(2 * i, 2 * i, tp)
+        att_self(2 * i + 1, 2 * i + 1, tp)
+        return carry
+
+    lax.fori_loop(0, 4, near_self, 0)
 
     relay_y(0)
-    start_y(2)
-
     kv_wait(p_sib, tp)
 
-    def near_range(lo, hi):
-        n = hi - lo
-
+    @pl.when(p_sib < p)
+    def _():
         def body(i, carry):
-            att_piece(i // n, i // n, tp, lo + i % n)
+            att_tile(2 * i, 2 * i, tp, p_sib, 1)
             return carry
 
-        lax.fori_loop(0, 8 * n, body, 0)
-
-    @pl.when(p_sib < p)
-    def _():
-        def body(h, carry):
-            att_piece(h, h, tp, p_sib)
-            return carry
-
-        lax.fori_loop(0, 8, body, 0)
-
-    relay_y(1)
-    start_y(3)
+        lax.fori_loop(0, 4, body, 0)
+
+    @pl.when(is_h)
+    def _():
+        kv_wait(cp, 0)
+        kv_copy(cp, 0, kvs.at[11], xn).start()
+        kv_copy(cp, 0, kvs.at[9], sib).start()
+
     relay_x(0)
 
     @pl.when(x_gets)
@@ -272,24 +283,26 @@
         kv_wait(p_xs, tp)
 
         def body(i, carry):
-            att_piece(i // 2, i // 2, tp, lax.min(p_x, p_xs) + i % 2)
+            att_tile(2 * i, 2 * i, tp, lax.min(p_x, p_xs), 2)
             return carry
 
-        lax.fori_loop(0, 16, body, 0)
+        lax.fori_loop(0, 4, body, 0)
 
     ready(0)
     kv_project(a_f[0], far)
     own_kv_sends(far, 1, True)
-
-    relay_y(2)
-    start_y(4)
-    relay_x(1)
+    for k in range(3, 5):
+        start_y(k)
+
+    def send_rest(k, carry):
+        start_y(k)
+        return carry
+
+    lax.fori_loop(5, N_ITEMS, send_rest, 0)
+    relay_y(1)
 
     @pl.when(is_h)
     def _():
-        kv_wait(cp, 0)
-        kv_copy(cp, 0, kvs.at[11], xn).start()
-        kv_copy(cp, 0, kvs.at[9], sib).start()
         kv_wait(cp_x, 0)
         kv_copy(cp_x, 0, kvs.at[12], sib).start()
 
@@ -298,6 +311,9 @@
         kv_wait(p_x, far)
         kv_copy(p_x, far, kvs.at[8], sib).start()
 
+    relay_y(2)
+    relay_x(1)
+
     kv_wait(p_sib, far)
 
     @pl.when(x_gets)
@@ -309,72 +325,89 @@
         kv_wait(cp_sib, 0)
         kv_wait(cp_xs, 0)
 
-    def far_q(j):
+    def far_pair(j, carry):
+        @pl.when(j == 2)
+        def _():
+            def body(i, c):
+                @pl.when(is_h)
+                def _():
+                    att_tile(2 * i, 2 * i, 1, 0, 4)
+
+                @pl.when(i < 3)
+                def _():
+                    ry(3 + i)
+
+                @pl.when(i > 0)
+                def _():
+                    rx(2 + i)
+
+                return c
+
+            lax.fori_loop(0, 4, body, 0)
+
+        rd = a_f.at[1 + j, pl.ds(cp_sib * 512, 512), :]
+        remote(rd, rd, d1s.at[1 + j], d1r.at[1 + j], sib).wait_recv()
+        rd2 = a_f.at[1 + j, pl.ds(cp_xs * 512, 512), :]
+        remote(rd2, rd2, d2s.at[1 + j], d2r.at[1 + j], sib).wait_recv()
         r = project(a_f[1 + j])
-        qb[8 + 2 * j] = r[:, 0:HD]
-        qb[9 + 2 * j] = r[:, HD:2 * HD]
-
-    def far_head(hf):
-        att_self(hf, 8 + hf, far)
-
-        def body(i, carry):
-            att_piece(hf, 8 + hf, far, i)
-            return carry
-
-        lax.fori_loop(0, p, body, 0)
-        finish_head(hf, 8 + hf)
-
-    def far_head_slot(hf, slot):
-        att_self(slot, 8 + hf, far)
-
-        def body(i, carry):
-            att_piece(slot, 8 + hf, far, i)
-            return carry
-
-        lax.fori_loop(0, p, body, 0)
-        finish_head(slot, 8 + hf)
-
-    ready(1)
-    far_q(0)
-
-    def far0(i, carry):
-        far_head_slot(i, 8 + i % 2)
-        return carry
-
-    lax.fori_loop(0, 2, far0, 0)
-
-    relay_y(3)
-    start_y(5)
-    start_y(6)
-    relay_x(2)
-
-    @pl.when(is_h)
-    def _():
-        kv_wait(cp, 1)
-        kv_copy(cp, 1, kvs.at[10], sib).start()
-        kv_wait(cp_x, 1)
-        kv_copy(cp_x, 1, kvs.at[13], sib).start()
-        kv_wait(cp_sib, 1)
-        kv_wait(cp_xs, 1)
-
-        def body(i, carry):
-            att_piece(i // 4, i // 4, 1, i % 4)
-            return carry
-
-        lax.fori_loop(0, 16, body, 0)
-
-    relay_y(4)
-    start_y(7)
-    start_y(8)
-    relay_x(3)
-
-    @pl.when(is_h)
-    def _():
-        def body(i, carry):
-            att_piece(i // 4, i // 4, 1, i % 4)
-            return carry
-
-        lax.fori_loop(16, 32, body, 0)
+        qi = 8 + 2 * j
+        qb[qi] = r[:, 0:HD]
+        qb[qi + 1] = r[:, HD:2 * HD]
+        att_self(8, qi, far)
+        att_self(9, qi + 1, far)
+
+        @pl.when(j >= 2)
+        def _():
+            ry(3 * j)
+
+        @pl.when(is_h)
+        def _():
+            att_tile(8, qi, far, 0, 4)
+
+        @pl.when(j == 0)
+        def _():
+            rx(2)
+
+        @pl.when(j == 1)
+        def _():
+            @pl.when(is_h)
+            def _():
+                kv_wait(cp, 1)
+                kv_copy(cp, 1, kvs.at[10], sib).start()
+                kv_wait(cp_x, 1)
+                kv_copy(cp_x, 1, kvs.at[13], sib).start()
+                kv_wait(cp_sib, 1)
+                kv_wait(cp_xs, 1)
+
+        @pl.when(j >= 2)
+        def _():
+            ry(3 * j + 1)
+            rx(3 * j)
+
+        lo = 4 * tp
+
+        @pl.when(p - lo >= 2)
+        def _():
+            att_tile(8, qi, far, lo, 2)
+
+        @pl.when((p - lo) % 2 == 1)
+        def _():
+            att_tile(8, qi, far, p - 1, 1)
+
+        @pl.when(j >= 2)
+        def _():
+            rx(3 * j + 1)
+            ry(3 * j + 2)
+
+        finish_head(8, qi)
+        finish_head(9, qi + 1)
+        return carry
+
+    lax.fori_loop(0, 4, far_pair, 0)
+
+    relay_y(12)
+    relay_x(8)
+    relay_x(11)
 
     def near_finish(h, carry):
         finish_head(h, h)
@@ -392,45 +425,14 @@
 
     lax.fori_loop(0, 4, near_out, 0)
 
-    def far_rest(i, carry):
-        hf = i + 2
-
-        @pl.when(i == 0)
-        def _():
-            relay_x(4)
-
-        @pl.when(i > 0)
-        def _():
-            relay_x(4 + i)
-
-        relay_y(5 + i)
-
-        @pl.when(i < 4)
-        def _():
-            start_y(9 + i)
-
-        @pl.when(i % 2 == 0)
-        def _():
-            j = hf // 2
-            rd = a_f.at[1 + j, pl.ds(cp_sib * 512, 512), :]
-            remote(rd, rd, d1s.at[1 + j], d1r.at[1 + j], sib).wait_recv()
-            rd2 = a_f.at[1 + j, pl.ds(cp_xs * 512, 512), :]
-            remote(rd2, rd2, d2s.at[1 + j], d2r.at[1 + j], sib).wait_recv()
-            far_q(j)
-
-        far_head_slot(hf, 8 + i % 2)
-        return carry
-
-    lax.fori_loop(0, 6, far_rest, 0)
-
-    def far_out(j, last):
-        ready(5 + 2 * j)
-        ready(6 + 2 * j)
+    def far_out(j, n, last):
+        for k in range(2 * j, 2 * j + 2 * n):
+            ready(5 + k)
 
         def body(t, carry):
             cols = pl.ds(pl.multiple_of(t * 512, 512), 512)
-            o_pair = jnp.concatenate([ob[8 + 2 * j], ob[9 + 2 * j]], axis=1)
-            w = jnp.concatenate([wo_f[2 * j, :, cols], wo_f[2 * j + 1, :, cols]], axis=0)
+            o_pair = jnp.concatenate([ob[8 + k] for k in range(2 * j, 2 * j + 2 * n)], axis=1)
+            w = jnp.concatenate([wo_f[k, :, cols] for k in range(2 * j, 2 * j + 2 * n)], axis=0)
             r = yacc[:, cols] + dot_nn(o_pair, w)
             if last:
                 out_ref[:, cols] = r.astype(BF16)
@@ -440,15 +442,10 @@
 
         lax.fori_loop(0, 4, body, 0)
 
-    relay_y(11)
-    relay_x(10)
-    far_out(0, False)
-    relay_y(12)
-    relay_x(11)
-    far_out(1, False)
+    far_out(0, 2, False)
     relay_x(12)
-    far_out(2, False)
-    far_out(3, True)
+    far_out(2, 1, False)
+    far_out(3, 1, True)
 
     for k in range(5):
         for c in y_send(k):

time: 143 us -> 115 us (0.80); the launches traced: 140 us -> 115 us
  Pallas kernels: 137 us -> 112 us
    pallas_call x1, Pallas kernels: 137 us -> 112 us  [local_layer(): pl.pallas_call(kernel, out_shape=jax.ShapeDtypeStruct((R, 2048), BF16), i...]
where the time goes in v2:
time: 115 us
  Pallas kernels  112 us (97%)
  local copies, waits for them, and re-layouts  3.16 us (3%)
    pallas_call x1, Pallas kernels, local_layer(): pl.pallas_call(kernel, out_shape=jax.ShapeDtypeStruct((R, 2048), BF16), i...  112 us
    unnamed x1, local copies, waits for them, and re-layouts  3.16 us

profile of v2, /device:TPU:5, one launch (start us, length us, event | category | flops | bytes accessed | tf_op | source)
XLA Modules:
  0.0 114.8 jit_solution(16414350126574502632)
XLA Ops:
  0.0 111.6 %attn_all.1 = bf16[512,2048]{1,0:T(8,128)(2,1)} custom-call(bf16[512,2048]{1,0:T(8,128)(2,1)} %x_hbm.1, bf16[2048,1024]{1,0:T(8,128)(2,1)} %wq_hbm.1, bf16[2048,128]{1,0:T(8,128)(2,1)} %wk_hbm.1, bf16[2048,128]{1,0:T(8,128)(2,1)} %wv_hbm.1, bf16[1024,2048]{1,0:T(8,128)(2,1)} %wo_hbm.1), custom_call_target="tpu_custom_call" | custom-call | tf_op jit(solution)/shard_map/attn_all/pallas_call | solution.py:504
  111.6 3.2 %copy.7 = bf16[512,2048]{1,0:T(8,128)(2,1)} copy(bf16[512,2048]{1,0:T(8,128)(2,1)} %attn_all.1) | data formatting | bytes 4194304

commit v3 on v2

--- a/solution.py
+++ b/solution.py
@@ -61,7 +61,7 @@
              load(2, wv_hbm, wkv_n.at[:, pl.ds(HD, HD)])]
     loads += [load(3 + j, wq_hbm.at[:, pl.ds(256 * j, 256)], wq_n.at[j]) for j in range(4)]
     loads += [load(7, wo_hbm, wo_n)]
-    for cpy in loads:
+    for cpy in loads[:3]:
         cpy.start()
 
     bar = pltpu.get_barrier_semaphore()
@@ -119,6 +119,11 @@
         for c in y_send(k):
             c.start()
 
+    def l_send(k):
+        @pl.when(is_l)
+        def _():
+            start_y(k)
+
     def relay_y(k):
         for c in y_send(k):
             c.wait_recv()
@@ -143,7 +148,7 @@
     def kv_wait(piece, e):
         kv_copy(piece, e, kvs.at[0], sib).wait_recv()
 
-    def own_kv_sends(e, slot, diag):
+    def own_kv_sends(e, slot):
         kv_copy(p, e, kvs.at[slot], sib).start()
 
         @pl.when(x_sends)
@@ -153,8 +158,6 @@
         @pl.when(is_l)
         def _():
             kv_copy(p, e, kvs.at[4 + slot], yn).start()
-            if diag:
-                kv_copy(p, e, kvs.at[6], dg).start()
 
     def project(w):
         return dot_nn(xs[...], w).astype(BF16)
@@ -182,18 +185,18 @@
         pr = jnp.concatenate([t.astype(BF16) for t in parts], axis=1)
         acc_st[slot] = acc_st[slot] * alpha + dot_nn(pr, v)
 
-    def att_self(slot, qi, e):
-        base = pl.multiple_of(p * R, R)
-        k = kvb[e, pl.ds(base, R), 0:HD]
-        v = kvb[e, pl.ds(base, R), HD:2 * HD]
-        row = lax.broadcasted_iota(jnp.int32, (256, 256), 0)
-        col = lax.broadcasted_iota(jnp.int32, (256, 256), 1)
-        s = dot_nt(qb[qi, 0:256, :], k[0:256])
-        soft_new(slot, slice(0, 256), jnp.where(row >= col, s, -jnp.inf), v[0:256])
-        row2 = lax.broadcasted_iota(jnp.int32, (256, 512), 0) + 256
-        col2 = lax.broadcasted_iota(jnp.int32, (256, 512), 1)
-        s = dot_nt(qb[qi, 256:512, :], k)
-        soft_new(slot, slice(256, 512), jnp.where(row2 >= col2, s, -jnp.inf), v)
+    def att_own(slot, qi, e, n, heads):
+        base = pl.multiple_of((p + 1 - n) * R, R)
+        k = kvb[e, pl.ds(base, n * R), 0:HD]
+        v = kvb[e, pl.ds(base, n * R), HD:2 * HD]
+        row = lax.broadcasted_iota(jnp.int32, (R, R), 0)
+        col = lax.broadcasted_iota(jnp.int32, (R, R), 1)
+        for u in range(heads):
+            s = dot_nt(qb[qi + u], k)
+            own = jnp.where(row >= col, s[:, (n - 1) * R:], -jnp.inf)
+            if n > 1:
+                own = jnp.concatenate([s[:, :(n - 1) * R], own], axis=1)
+            soft_new(slot + u, slice(0, R), own, v)
 
     def att_tile(slot, qi, e, piece, n_pieces):
         base = pl.multiple_of(piece * R, R)
@@ -231,18 +234,18 @@
         dyn(k, fn)
 
     start_y(0)
+    for cpy in loads[3:7]:
+        cpy.start()
     loads[0].wait()
     loads[1].wait()
     loads[2].wait()
     kv_project(wkv_n[...], tp)
-    own_kv_sends(tp, 0, False)
+    own_kv_sends(tp, 0)
     start_y(1)
-    start_y(2)
-
-    for j in range(4):
-        loads[3 + j].wait()
+    loads[7].start()
 
     def q_near(j, carry):
+        load(3 + j, wq_hbm.at[:, pl.ds(pl.multiple_of(256 * j, 256), 256)], wq_n.at[j]).wait()
         r = project(wq_n[j])
         qb[2 * j] = r[:, 0:HD]
         qb[2 * j + 1] = r[:, HD:2 * HD]
@@ -251,13 +254,21 @@
     lax.fori_loop(0, 4, q_near, 0)
 
     def near_self(i, carry):
-        att_self(2 * i, 2 * i, tp)
-        att_self(2 * i + 1, 2 * i + 1, tp)
-        return carry
-
-    lax.fori_loop(0, 4, near_self, 0)
-
-    relay_y(0)
+        att_own(4 * i, 4 * i, tp, 1, 4)
+
+        @pl.when(i == 0)
+        def _():
+            relay_y(0)
+
+        return carry
+
+    lax.fori_loop(0, 2, near_self, 0)
+
+    @pl.when(x_gets)
+    def _():
+        kv_wait(p_x, tp)
+        kv_copy(p_x, tp, kvs.at[7], sib).start()
+
     kv_wait(p_sib, tp)
 
     @pl.when(p_sib < p)
@@ -274,76 +285,124 @@
         kv_copy(cp, 0, kvs.at[11], xn).start()
         kv_copy(cp, 0, kvs.at[9], sib).start()
 
-    relay_x(0)
-
     @pl.when(x_gets)
     def _():
-        kv_wait(p_x, tp)
-        kv_copy(p_x, tp, kvs.at[7], sib).start()
         kv_wait(p_xs, tp)
 
-        def body(i, carry):
+    def near_x(i, carry):
+        @pl.when(x_gets)
+        def _():
             att_tile(2 * i, 2 * i, tp, lax.min(p_x, p_xs), 2)
-            return carry
-
-        lax.fori_loop(0, 4, body, 0)
-
-    ready(0)
-    kv_project(a_f[0], far)
-    own_kv_sends(far, 1, True)
-    for k in range(3, 5):
-        start_y(k)
-
-    def send_rest(k, carry):
-        start_y(k)
-        return carry
-
-    lax.fori_loop(5, N_ITEMS, send_rest, 0)
-    relay_y(1)
+
+        @pl.when(i == 0)
+        def _():
+            relay_x(0)
+
+        @pl.when(i == 1)
+        def _():
+            ready(0)
+            kv_project(a_f[0], far)
+            own_kv_sends(far, 1)
+
+        @pl.when(i == 3)
+        def _():
+            relay_y(1)
+
+            @pl.when(is_h)
+            def _():
+                for k in range(2, 5):
+                    start_y(k)
+
+                def send_rest(k, c):
+                    start_y(k)
+                    return c
+
+                lax.fori_loop(5, N_ITEMS, send_rest, 0)
+
+        return carry
+
+    lax.fori_loop(0, 4, near_x, 0)
+    kv_wait(p_sib, far)
 
     @pl.when(is_h)
     def _():
         kv_wait(cp_x, 0)
         kv_copy(cp_x, 0, kvs.at[12], sib).start()
+        kv_wait(cp_sib, 0)
+        kv_wait(cp, 1)
+        kv_copy(cp, 1, kvs.at[10], sib).start()
+        kv_wait(cp_sib, 1)
+
+    def near_l(i, carry):
+        @pl.when(is_h)
+        def _():
+            att_tile(2 * i, 2 * i, 1, 2 * xc, 2)
+
+        @pl.when((i == 0) & is_l)
+        def _():
+            kv_copy(p, far, kvs.at[5], yn).wait_send()
+            kv_copy(p, far, kvs.at[6], dg).start()
+            start_y(2)
+
+        @pl.when((i == 0) & x_gets)
+        def _():
+            kv_wait(p_x, far)
+            kv_copy(p_x, far, kvs.at[8], sib).start()
+
+        @pl.when((i == 2) & is_h)
+        def _():
+            kv_wait(cp_x, 1)
+            kv_copy(cp_x, 1, kvs.at[13], sib).start()
+
+        @pl.when(i == 3)
+        def _():
+            l_send(3)
+            relay_x(1)
+
+        return carry
+
+    lax.fori_loop(0, 4, near_l, 0)
 
     @pl.when(x_gets)
     def _():
-        kv_wait(p_x, far)
-        kv_copy(p_x, far, kvs.at[8], sib).start()
-
-    relay_y(2)
-    relay_x(1)
-
-    kv_wait(p_sib, far)
-
-    @pl.when(x_gets)
-    def _():
         kv_wait(p_xs, far)
 
     @pl.when(is_h)
     def _():
-        kv_wait(cp_sib, 0)
         kv_wait(cp_xs, 0)
 
     def far_pair(j, carry):
-        @pl.when(j == 2)
-        def _():
+        @pl.when(j == 1)
+        def _():
+            @pl.when(is_h)
+            def _():
+                kv_wait(cp_xs, 1)
+
             def body(i, c):
                 @pl.when(is_h)
                 def _():
-                    att_tile(2 * i, 2 * i, 1, 0, 4)
-
-                @pl.when(i < 3)
+                    att_tile(2 * i, 2 * i, 1, 2 - 2 * xc, 2)
+
+                @pl.when(i == 1)
                 def _():
-                    ry(3 + i)
-
-                @pl.when(i > 0)
-                def _():
-                    rx(2 + i)
+                    ry(3)
+                    l_send(5)
+                    l_send(6)
+                    rx(2)
 
                 return c
 
             lax.fori_loop(0, 4, body, 0)
+
+        @pl.when(j == 2)
+        def _():
+            ry(6)
+            l_send(9)
+            rx(4)
+
+        @pl.when(j == 3)
+        def _():
+            rx(7)
 
         rd = a_f.at[1 + j, pl.ds(cp_sib * 512, 512), :]
         remote(rd, rd, d1s.at[1 + j], d1r.at[1 + j], sib).wait_recv()
@@ -353,51 +412,53 @@
         qi = 8 + 2 * j
         qb[qi] = r[:, 0:HD]
         qb[qi + 1] = r[:, HD:2 * HD]
-        att_self(8, qi, far)
-        att_self(9, qi + 1, far)
-
-        @pl.when(j >= 2)
-        def _():
-            ry(3 * j)
+        for n in range(1, 5):
+            @pl.when(p - 4 * tp + 1 == n)
+            def _():
+                att_own(8, qi, far, n, 2)
+
+        @pl.when(j == 0)
+        def _():
+            ry(2)
+            l_send(4)
+
+        @pl.when(j == 1)
+        def _():
+            ry(4)
+            l_send(7)
+            rx(3)
+
+        @pl.when(j == 2)
+        def _():
+            ry(7)
+            l_send(10)
+            rx(5)
+
+        @pl.when(j == 3)
+        def _():
+            ry(9)
+            l_send(12)
+            rx(8)
 
         @pl.when(is_h)
         def _():
             att_tile(8, qi, far, 0, 4)
 
-        @pl.when(j == 0)
-        def _():
-            rx(2)
-
         @pl.when(j == 1)
         def _():
-            @pl.when(is_h)
-            def _():
-                kv_wait(cp, 1)
-                kv_copy(cp, 1, kvs.at[10], sib).start()
-                kv_wait(cp_x, 1)
-                kv_copy(cp_x, 1, kvs.at[13], sib).start()
-                kv_wait(cp_sib, 1)
-                kv_wait(cp_xs, 1)
-
-        @pl.when(j >= 2)
-        def _():
-            ry(3 * j + 1)
-            rx(3 * j)
-
-        lo = 4 * tp
-
-        @pl.when(p - lo >= 2)
-        def _():
-            att_tile(8, qi, far, lo, 2)
-
-        @pl.when((p - lo) % 2 == 1)
-        def _():
-            att_tile(8, qi, far, p - 1, 1)
-
-        @pl.when(j >= 2)
-        def _():
-            rx(3 * j + 1)
-            ry(3 * j + 2)
+            ry(5)
+            l_send(8)
+
+        @pl.when(j == 2)
+        def _():
+            rx(6)
+            ry(8)
+            l_send(11)
+
+        @pl.when(j == 3)
+        def _():
+            ry(10)
+            rx(9)
 
         finish_head(8, qi)
         finish_head(9, qi + 1)
@@ -405,47 +466,44 @@
 
     lax.fori_loop(0, 4, far_pair, 0)
 
-    relay_y(12)
-    relay_x(8)
-    relay_x(11)
-
     def near_finish(h, carry):
         finish_head(h, h)
         return carry
 
     lax.fori_loop(0, 8, near_finish, 0)
+    relay_y(11)
+    relay_x(10)
 
     loads[7].wait()
-
-    def near_out(t, carry):
+    for k in range(4):
+        ready(5 + k)
+
+    def out_first(t, carry):
+        cols = pl.ds(pl.multiple_of(t * 256, 256), 256)
+        o_all = jnp.concatenate([ob[i] for i in range(12)], axis=1)
+        w = jnp.concatenate([wo_n[:, cols]] + [wo_f[k, :, cols] for k in range(4)], axis=0)
+        yacc[:, cols] = dot_nn(o_all, w)
+
+        @pl.when(t == 3)
+        def _():
+            relay_y(12)
+            relay_x(11)
+
+        return carry
+
+    lax.fori_loop(0, 8, out_first, 0)
+    relay_x(12)
+    for k in range(4, 8):
+        ready(5 + k)
+
+    def out_last(t, carry):
         cols = pl.ds(pl.multiple_of(t * 512, 512), 512)
-        o_all = jnp.concatenate([ob[i] for i in range(8)], axis=1)
-        yacc[:, cols] = dot_nn(o_all, wo_n[:, cols])
-        return carry
-
-    lax.fori_loop(0, 4, near_out, 0)
-
-    def far_out(j, n, last):
-        for k in range(2 * j, 2 * j + 2 * n):
-            ready(5 + k)
-
-        def body(t, carry):
-            cols = pl.ds(pl.multiple_of(t * 512, 512), 512)
-            o_pair = jnp.concatenate([ob[8 + k] for k in range(2 * j, 2 * j + 2 * n)], axis=1)
-            w = jnp.concatenate([wo_f[k, :, cols] for k in range(2 * j, 2 * j + 2 * n)], axis=0)
-            r = yacc[:, cols] + dot_nn(o_pair, w)
-            if last:
-                out_ref[:, cols] = r.astype(BF16)
-            else:
-                yacc[:, cols] = r
-            return carry
-
-        lax.fori_loop(0, 4, body, 0)
-
-    far_out(0, 2, False)
-    relay_x(12)
-    far_out(2, 1, False)
-    far_out(3, 1, True)
+        o_last = jnp.concatenate([ob[12 + k] for k in range(4)], axis=1)
+        w = jnp.concatenate([wo_f[4 + k, :, cols] for k in range(4)], axis=0)
+        out_ref[:, cols] = (yacc[:, cols] + dot_nn(o_last, w)).astype(BF16)
+        return carry
+
+    lax.fori_loop(0, 4, out_last, 0)
 
     for k in range(5):
         for c in y_send(k):
@@ -483,7 +541,6 @@
     @pl.when(is_l)
     def _():
         sent(p, tp, 4, yn)
-        sent(p, far, 5, yn)
         sent(p, far, 6, dg)
 
     @pl.when(is_h)
@@ -503,7 +560,7 @@
         dma = pltpu.SemaphoreType.DMA
         return pl.pallas_call(
             kernel,
-            out_shape=jax.ShapeDtypeStruct((R, 2048), BF16),
+            out_shape=pltpu.VMEM((R, 2048), BF16),
             in_specs=[anyspec] * 5,
             out_specs=pl.BlockSpec(memory_space=pltpu.VMEM),
             scratch_shapes=[
@@ -528,7 +585,7 @@
                 dma((8, 2)), dma((14,)),
             ],
             compiler_params=pltpu.CompilerParams(
-                collective_id=0, has_side_effects=True, vmem_limit_bytes=62 * 1024 * 1024),
+                collective_id=0, has_side_effects=True, vmem_limit_bytes=58 * 1024 * 1024),
             name="attn_all",
         )(x_loc, w_q, w_k, w_v, w_o)
 

time: 115 us -> 95 us (0.83)
  Pallas kernels: 112 us -> 93.6 us
  local copies, waits for them, and re-layouts: 3.16 us -> 1.32 us
    pallas_call x1, Pallas kernels: 112 us -> 93.6 us  [local_layer(): pl.pallas_call(kernel, out_shape=pltpu.VMEM((R, 2048), BF16), in_specs=[a...]
    unnamed x1, local copies, waits for them, and re-layouts: 3.16 us -> 1.32 us
where the time goes in v3:
time: 95 us; the launch traced here: 94.9 us
  Pallas kernels  93.6 us (99%)
  local copies, waits for them, and re-layouts  1.32 us (1%)
    pallas_call x1, Pallas kernels, local_layer(): pl.pallas_call(kernel, out_shape=pltpu.VMEM((R, 2048), BF16), in_specs=[a...  93.6 us

profile of v3, /device:TPU:5, one launch (start us, length us, event | category | flops | bytes accessed | tf_op | source)
XLA Modules:
  0.0 94.9 jit_solution(14003664293358692908)
XLA Ops:
  0.0 93.6 %attn_all.1 = bf16[512,2048]{1,0:T(8,128)(2,1)S(1)} custom-call(bf16[512,2048]{1,0:T(8,128)(2,1)} %x_hbm.1, bf16[2048,1024]{1,0:T(8,128)(2,1)} %wq_hbm.1, bf16[2048,128]{1,0:T(8,128)(2,1)} %wk_hbm.1, bf16[2048,128]{1,0:T(8,128)(2,1)} %wv_hbm.1, bf16[1024,2048]{1,0:T(8,128)(2,1)} %wo_hbm.1), custom_call_target="tpu_custom_call" | custom-call | tf_op jit(solution)/shard_map/attn_all/pallas_call | solution.py:561
  93.6 1.3 %copy.7 = bf16[512,2048]{1,0:T(8,128)(2,1)} copy(bf16[512,2048]{1,0:T(8,128)(2,1)S(1)} %attn_all.1) | data formatting | bytes 4194304

commit v4 on v3

--- a/solution.py
+++ b/solution.py
@@ -38,7 +38,6 @@
     sib = (dp, tp, cp_sib)
     xn = (dp, tp, cp_x)
     yn = (dp, 1 - tp, cp)
-    dg = (dp, 1 - tp, cp_x)
     far = 1 - tp
 
     def piece_of(c):
@@ -65,9 +64,9 @@
         cpy.start()
 
     bar = pltpu.get_barrier_semaphore()
-    for dev in (sib, xn, yn, dg):
+    for dev in (sib, xn, yn):
         pl.semaphore_signal(bar, 1, device_id=dev, device_id_type=MESH)
-    pl.semaphore_wait(bar, 4)
+    pl.semaphore_wait(bar, 3)
 
     def remote(src, dst, ss, rs, dev):
         return pltpu.make_async_remote_copy(src, dst, ss, rs, device_id=dev, device_id_type=MESH)
@@ -119,10 +118,15 @@
         for c in y_send(k):
             c.start()
 
-    def l_send(k):
-        @pl.when(is_l)
-        def _():
+    def send_rest():
+        for k in range(2, 5):
             start_y(k)
+
+        def body(k, carry):
+            start_y(k)
+            return carry
+
+        lax.fori_loop(5, N_ITEMS, body, 0)
 
     def relay_y(k):
         for c in y_send(k):
@@ -155,6 +159,7 @@
         def _():
             kv_copy(p, e, kvs.at[2 + slot], xn).start()
 
+    def own_kv_down(e, slot):
         @pl.when(is_l)
         def _():
             kv_copy(p, e, kvs.at[4 + slot], yn).start()
@@ -173,7 +178,8 @@
         parts = [exp_scaled(s[:, t:t + 128] - m) for t in range(0, s.shape[1], 128)]
         m_st[slot, rows, :] = jnp.broadcast_to(m, (m.shape[0], 128))
         l_st[slot, rows, :] = functools.reduce(jnp.add, parts)
-        acc_st[slot, rows, :] = dot_nn(jnp.concatenate([t.astype(BF16) for t in parts], axis=1), v)
+        pr = jnp.concatenate([t.astype(BF16) for t in parts], axis=1)
+        acc_st[slot, rows, :] = acc_st[slot, rows, :] + dot_nn(pr, v)
 
     def soft_add(slot, s, v):
         m_old = m_st[slot]
@@ -192,6 +198,7 @@
         row = lax.broadcasted_iota(jnp.int32, (R, R), 0)
         col = lax.broadcasted_iota(jnp.int32, (R, R), 1)
         for u in range(heads):
+            acc_st[slot + u] = jnp.zeros((R, HD), F32)
             s = dot_nt(qb[qi + u], k)
             own = jnp.where(row >= col, s[:, (n - 1) * R:], -jnp.inf)
             if n > 1:
@@ -241,7 +248,6 @@
     loads[2].wait()
     kv_project(wkv_n[...], tp)
     own_kv_sends(tp, 0)
-    start_y(1)
     loads[7].start()
 
     def q_near(j, carry):
@@ -259,6 +265,8 @@
         @pl.when(i == 0)
         def _():
             relay_y(0)
+            own_kv_down(tp, 0)
+            start_y(1)
 
         return carry
 
@@ -289,35 +297,24 @@
     def _():
         kv_wait(p_xs, tp)
 
+    relay_x(0)
+
     def near_x(i, carry):
         @pl.when(x_gets)
         def _():
             att_tile(2 * i, 2 * i, tp, lax.min(p_x, p_xs), 2)
 
         @pl.when(i == 0)
-        def _():
-            relay_x(0)
-
-        @pl.when(i == 1)
         def _():
             ready(0)
             kv_project(a_f[0], far)
             own_kv_sends(far, 1)
+            own_kv_down(far, 1)
+            send_rest()
 
         @pl.when(i == 3)
         def _():
             relay_y(1)
-
-            @pl.when(is_h)
-            def _():
-                for k in range(2, 5):
-                    start_y(k)
-
-                def send_rest(k, c):
-                    start_y(k)
-                    return c
-
-                lax.fori_loop(5, N_ITEMS, send_rest, 0)
 
         return carry
 
@@ -330,6 +327,7 @@
         kv_copy(cp_x, 0, kvs.at[12], sib).start()
         kv_wait(cp_sib, 0)
         kv_wait(cp, 1)
+        kv_copy(cp, 1, kvs.at[6], xn).start()
         kv_copy(cp, 1, kvs.at[10], sib).start()
         kv_wait(cp_sib, 1)
 
@@ -338,26 +336,15 @@
         def _():
             att_tile(2 * i, 2 * i, 1, 2 * xc, 2)
 
-        @pl.when((i == 0) & is_l)
-        def _():
-            kv_copy(p, far, kvs.at[5], yn).wait_send()
-            kv_copy(p, far, kvs.at[6], dg).start()
-            start_y(2)
-
         @pl.when((i == 0) & x_gets)
         def _():
             kv_wait(p_x, far)
             kv_copy(p_x, far, kvs.at[8], sib).start()
 
-        @pl.when((i == 2) & is_h)
-        def _():
-            kv_wait(cp_x, 1)
-            kv_copy(cp_x, 1, kvs.at[13], sib).start()
-
         @pl.when(i == 3)
         def _():
-            l_send(3)
             relay_x(1)
+            relay_y(2)
 
         return carry
 
@@ -370,6 +357,13 @@
     @pl.when(is_h)
     def _():
         kv_wait(cp_xs, 0)
+
+    def events(j, table):
+        for jj, evs in table.items():
+            @pl.when(j == jj)
+            def _():
+                for kind, k in evs:
+                    (ry if kind == "y" else rx)(k)
 
     def far_pair(j, carry):
         @pl.when(j == 1)
@@ -385,24 +379,16 @@
 
                 @pl.when(i == 1)
                 def _():
-                    ry(3)
-                    l_send(5)
-                    l_send(6)
-                    rx(2)
+                    ry(4)
+
+                @pl.when(i == 3)
+                def _():
+                    ry(5)
+                    rx(3)
 
                 return c
 
             lax.fori_loop(0, 4, body, 0)
-
-        @pl.when(j == 2)
-        def _():
-            ry(6)
-            l_send(9)
-            rx(4)
-
-        @pl.when(j == 3)
-        def _():
-            rx(7)
 
         rd = a_f.at[1 + j, pl.ds(cp_sib * 512, 512), :]
         remote(rd, rd, d1s.at[1 + j], d1r.at[1 + j], sib).wait_recv()
@@ -417,49 +403,24 @@
             def _():
                 att_own(8, qi, far, n, 2)
 
-        @pl.when(j == 0)
-        def _():
-            ry(2)
-            l_send(4)
-
-        @pl.when(j == 1)
-        def _():
-            ry(4)
-            l_send(7)
-            rx(3)
-
-        @pl.when(j == 2)
-        def _():
-            ry(7)
-            l_send(10)
-            rx(5)
-
-        @pl.when(j == 3)
-        def _():
-            ry(9)
-            l_send(12)
-            rx(8)
+        @pl.when((j == 0) & is_h)
+        def _():
+            kv_wait(cp_x, 1)
+            kv_copy(cp_x, 1, kvs.at[13], sib).start()
+
+        events(j, {0: [("y", 3)],
+                   1: [("y", 6), ("y", 7), ("x", 4)],
+                   2: [("y", 9), ("x", 6)],
+                   3: [("y", 12), ("x", 8), ("x", 9)]})
 
         @pl.when(is_h)
         def _():
             att_tile(8, qi, far, 0, 4)
 
-        @pl.when(j == 1)
-        def _():
-            ry(5)
-            l_send(8)
-
-        @pl.when(j == 2)
-        def _():
-            rx(6)
-            ry(8)
-            l_send(11)
-
-        @pl.when(j == 3)
-        def _():
-            ry(10)
-            rx(9)
-
+        events(j, {0: [("x", 2)],
+                   1: [("y", 8), ("x", 5)],
+                   2: [("y", 10), ("y", 11), ("x", 7)],
+                   3: [("x", 10)]})
         finish_head(8, qi)
         finish_head(9, qi + 1)
         return carry
@@ -471,8 +432,6 @@
         return carry
 
     lax.fori_loop(0, 8, near_finish, 0)
-    relay_y(11)
-    relay_x(10)
 
     loads[7].wait()
     for k in range(4):
@@ -484,15 +443,17 @@
         w = jnp.concatenate([wo_n[:, cols]] + [wo_f[k, :, cols] for k in range(4)], axis=0)
         yacc[:, cols] = dot_nn(o_all, w)
 
-        @pl.when(t == 3)
-        def _():
-            relay_y(12)
+        @pl.when(t == 0)
+        def _():
             relay_x(11)
 
+        @pl.when(t == 5)
+        def _():
+            relay_x(12)
+
         return carry
 
     lax.fori_loop(0, 8, out_first, 0)
-    relay_x(12)
     for k in range(4, 8):
         ready(5 + k)
 
@@ -541,13 +502,14 @@
     @pl.when(is_l)
     def _():
         sent(p, tp, 4, yn)
-        sent(p, far, 6, dg)
+        sent(p, far, 5, yn)
 
     @pl.when(is_h)
     def _():
         sent(cp, 0, 9, sib)
         sent(cp, 1, 10, sib)
         sent(cp, 0, 11, xn)
+        sent(cp, 1, 6, xn)
         sent(cp_x, 0, 12, sib)
         sent(cp_x, 1, 13, sib)
 

time: 95 us -> 85.3 us (0.90)
  Pallas kernels: 93.6 us -> 83.9 us
    pallas_call x1, Pallas kernels: 93.6 us -> 83.9 us  [local_layer(): pl.pallas_call(kernel, out_shape=pltpu.VMEM((R, 2048), BF16), in_specs=[a...]
where the time goes in v4:
time: 85.3 us; the launch traced here: 85.2 us
  Pallas kernels  83.9 us (98%)
  local copies, waits for them, and re-layouts  1.32 us (2%)
    pallas_call x1, Pallas kernels, local_layer(): pl.pallas_call(kernel, out_shape=pltpu.VMEM((R, 2048), BF16), in_specs=[a...  83.9 us

profile of v4, /device:TPU:5, one launch (start us, length us, event | category | flops | bytes accessed | tf_op | source)
XLA Modules:
  0.0 85.2 jit_solution(15907543676996919040)
XLA Ops:
  0.0 83.9 %attn_all.1 = bf16[512,2048]{1,0:T(8,128)(2,1)S(1)} custom-call(bf16[512,2048]{1,0:T(8,128)(2,1)} %x_hbm.1, bf16[2048,1024]{1,0:T(8,128)(2,1)} %wq_hbm.1, bf16[2048,128]{1,0:T(8,128)(2,1)} %wk_hbm.1, bf16[2048,128]{1,0:T(8,128)(2,1)} %wv_hbm.1, bf16[1024,2048]{1,0:T(8,128)(2,1)} %wo_hbm.1), custom_call_target="tpu_custom_call" | custom-call | tf_op jit(solution)/shard_map/attn_all/pallas_call | solution.py:523
  83.9 1.3 %copy.7 = bf16[512,2048]{1,0:T(8,128)(2,1)} copy(bf16[512,2048]{1,0:T(8,128)(2,1)S(1)} %attn_all.1) | data formatting | bytes 4194304

commit v5 on v4

--- a/solution.py
+++ b/solution.py
@@ -454,18 +454,6 @@
         return carry
 
     lax.fori_loop(0, 8, out_first, 0)
-    for k in range(4, 8):
-        ready(5 + k)
-
-    def out_last(t, carry):
-        cols = pl.ds(pl.multiple_of(t * 512, 512), 512)
-        o_last = jnp.concatenate([ob[12 + k] for k in range(4)], axis=1)
-        w = jnp.concatenate([wo_f[4 + k, :, cols] for k in range(4)], axis=0)
-        out_ref[:, cols] = (yacc[:, cols] + dot_nn(o_last, w)).astype(BF16)
-        return carry
-
-    lax.fori_loop(0, 4, out_last, 0)
-
     for k in range(5):
         for c in y_send(k):
             c.wait_send()
@@ -481,7 +469,7 @@
         d2_fwd(k).wait_send()
         return carry
 
-    lax.fori_loop(5, N_ITEMS, drain, 0)
+    lax.fori_loop(5, 11, drain, 0)
 
     def sent(piece, e, slot, dev):
         kv_copy(piece, e, kvs.at[slot], dev).wait_send()
@@ -512,6 +500,20 @@
         sent(cp, 1, 6, xn)
         sent(cp_x, 0, 12, sib)
         sent(cp_x, 1, 13, sib)
+
+    for k in range(4, 8):
+        ready(5 + k)
+
+    def out_last(t, carry):
+        cols = pl.ds(pl.multiple_of(t * 512, 512), 512)
+        o_last = jnp.concatenate([ob[12 + k] for k in range(4)], axis=1)
+        w = jnp.concatenate([wo_f[4 + k, :, cols] for k in range(4)], axis=0)
+        out_ref[:, cols] = (yacc[:, cols] + dot_nn(o_last, w)).astype(BF16)
+        return carry
+
+    lax.fori_loop(0, 4, out_last, 0, unroll=True)
+
+    lax.fori_loop(11, N_ITEMS, drain, 0)
 
 
 def solution(mesh):

time: 85.3 us -> 84.7 us (level)
  no operation moved by 1% of the time
where the time goes in v5:
time: 84.7 us; the launch traced here: 84.6 us
  Pallas kernels  83.3 us (98%)
  local copies, waits for them, and re-layouts  1.32 us (2%)
    pallas_call x1, Pallas kernels, local_layer(): pl.pallas_call(kernel, out_shape=pltpu.VMEM((R, 2048), BF16), in_specs=[a...  83.3 us

profile of v5, /device:TPU:5, one launch (start us, length us, event | category | flops | bytes accessed | tf_op | source)
XLA Modules:
  0.0 84.6 jit_solution(13424106286599855588)
XLA Ops:
  0.0 83.3 %attn_all.1 = bf16[512,2048]{1,0:T(8,128)(2,1)S(1)} custom-call(bf16[512,2048]{1,0:T(8,128)(2,1)} %x_hbm.1, bf16[2048,1024]{1,0:T(8,128)(2,1)} %wq_hbm.1, bf16[2048,128]{1,0:T(8,128)(2,1)} %wk_hbm.1, bf16[2048,128]{1,0:T(8,128)(2,1)} %wv_hbm.1, bf16[1024,2048]{1,0:T(8,128)(2,1)} %wo_hbm.1), custom_call_target="tpu_custom_call" | custom-call | tf_op jit(solution)/shard_map/attn_all/pallas_call | solution.py:525
  83.3 1.3 %copy.7 = bf16[512,2048]{1,0:T(8,128)(2,1)} copy(bf16[512,2048]{1,0:T(8,128)(2,1)S(1)} %attn_all.1) | data formatting | bytes 4194304
